TPU v7x, 32 devices: a whole 2x2x4 slice. The times are simulated.
32 devices in a mesh: shard: 8 (over z, y), model: 4 (over x, core).
Axes of the slice: x: 2, y: 2, z: 4, core: 2. Of those that a mesh axis runs over, the one named last changes fastest.
Arguments:
- one_gate: float32 [2048, 8192], P('shard', 'model'), may hold values from -0.1875 to 0.1875
- other_gate: float32 [2048, 8192], P('shard', 'model'), may hold values from -0.125 to 0.125
- one_up: float32 [2048, 8192], P('shard', 'model'), may hold values from -0.1875 to 0.1875
- other_up: float32 [2048, 8192], P('shard', 'model'), may hold values from -0.125 to 0.125
- mix_share: float32 [2048], P('shard'), may hold values from 0.2 to 0.8
- norm_train: float32 [2048], P(('shard', 'model')), may hold values from 0.25 to 1.75
- norm_step: float32 [2048], P(('shard', 'model')), may hold values from -0.3 to 0.3
Outputs:
- final_gate: bfloat16 [2048, 8192], P(None, 'model')
- final_up: bfloat16 [2048, 8192], P(None, 'model')
- column_gate: float32 [8192], P('model')
- column_up: float32 [8192], P('model')
- serve_norm: bfloat16 [2048], replicated
All inputs are finite; a program needn't handle non-finite values. Where the computation divides by a largest or mean magnitude, that divisor is 1e-20 or more.
Results may differ from a plain program's by a relative error of at most 0.001.
Values may be sent and summed in bfloat16 or wider, within the bound.
A program may use at most 128 MiB of HBM per device.

v0:
```python
import jax
import jax.numpy as jnp
from jax import lax
from jax.sharding import PartitionSpec as P


def local(one_gate, other_gate, one_up, other_up, mix_share, norm_train, norm_step):
    result_gate = mix_share[:, None] * one_gate + (1.0 - mix_share[:, None]) * other_gate
    result_up = mix_share[:, None] * one_up + (1.0 - mix_share[:, None]) * other_up
    column_gate, column_up = lax.pmax(
        (jnp.max(jnp.abs(result_gate), axis=0), jnp.max(jnp.abs(result_up), axis=0)), "shard"
    )
    narrow_gate, narrow_up = (
        (result_gate / column_gate).astype(jnp.bfloat16),
        (result_up / column_up).astype(jnp.bfloat16),
    )
    final_gate, final_up = (
        lax.all_gather(narrow_gate, "shard", axis=0, tiled=True),
        lax.all_gather(narrow_up, "shard", axis=0, tiled=True),
    )
    serve_norm = lax.all_gather(
        (norm_train + norm_step).astype(jnp.bfloat16), ("shard", "model"), axis=0, tiled=True
    )
    return (final_gate, final_up, column_gate, column_up, serve_norm)


def solution(mesh):
    placed = (
        P("shard", "model"),
        P("shard", "model"),
        P("shard", "model"),
        P("shard", "model"),
        P("shard"),
        P(("shard", "model")),
        P(("shard", "model")),
    )
    return jax.shard_map(
        local,
        mesh=mesh,
        in_specs=placed,
        out_specs=(P(None, "model"), P(None, "model"), P("model"), P("model"), P()),
        check_vma=False,
    )
```

profile of v0, /device:TPU:0, one launch (start us, length us, event | category | flops | bytes accessed | tf_op | source)
XLA Modules:
  0.0 328.6 jit_solution(4167982296349266653)
XLA Ops:
  7.2 0.0 all-gather.3.cloned.1.call-start
  7.2 0.7 broadcast_subtract_fusion
  7.9 0.0 copy-start
  7.9 0.0 copy-start.1
  7.9 4.4 %abs_reduce_fusion = (f32[2048]{0:T(1024)S(1)}, f32[2048]{0:T(1024)S(1)}) fusion(f32[256,2048]{1,0:T(8,128)} %param.10, f32[256]{0:T(256)S(1)} %broadcast_subtract_fusion, f32[256,2048]{1,0:T(8,128)} %param.9, f32[256]{0:T(256)} %param.11, f32[256,2048]{1,0:T(8,128)} %param.8, f32[256,2048]{1,0:T(8,128)} %param.7), kind=kLoop, calls=%fused_computation.1 | loop fusion | flops 5238784 | bytes 8407040 | tf_op jit(solution)/shard_map/reduce_max | solution.py:11
  12.3 38.9 %all-reduce.1 = (f32[2048]{0:T(1024)S(1)}, f32[2048]{0:T(1024)S(1)}) all-reduce(f32[2048]{0:T(1024)S(1)} %get-tuple-element.6, f32[2048]{0:T(1024)S(1)} %get-tuple-element.5), channel_id=1, replica_groups=mesh['shard'=8,'model'=4] {'shard'}, use_global_device_ids=true, to_apply=%region_1.0 | all-reduce | flops 4096 | bytes 32768 | tf_op jit(solution)/shard_map/pmax | solution.py:10
  51.1 0.0 copy-start.2
  51.1 0.0 copy-start.3
  51.1 0.0 copy-done
  51.2 0.0 copy-done.1
  51.2 5.4 %divide_convert_fusion = (bf16[256,2048]{1,0:T(8,128)(2,1)}, bf16[256,2048]{1,0:T(8,128)(2,1)}) fusion(f32[2048]{0:T(1024)S(1)} %get-tuple-element.19, f32[256,2048]{1,0:T(8,128)S(1)} %copy-done, f32[256]{0:T(256)S(1)} %broadcast_subtract_fusion, f32[256,2048]{1,0:T(8,128)} %param.9, f32[256]{0:T(256)S(1)} %copy-done.1, f32[2048]{0:T(1024)S(1)} %get-tuple-element.18, ...), kind=kLoop, calls=%fused_computation | loop fusion | flops 5242880 | bytes 10504192 | tf_op jit(solution)/shard_map/convert_element_type | solution.py:15
  56.5 0.0 copy-done.2
  56.5 0.0 copy-done.3
  56.5 0.0 copy-start.4
  56.5 0.0 copy-start.5
  56.5 0.0 all-gather.3.cloned.1.call-update
  56.6 0.0 all-gather.5.cloned.1.call-start
  56.6 0.7 all-gather.5.cloned.1.call-update
  57.3 0.0 copy-done.4
  57.3 0.0 copy-done.5
  57.4 0.2 dynamic-update-slice
  57.6 40.9 %all-reduce = bf16[2048]{0:T(1024)(128)(2,1)} all-reduce(bf16[2048]{0:T(1024)(128)(2,1)S(1)} %dynamic-update-slice), channel_id=1, replica_groups=mesh['shard'=8,'model'=4] {'shard','model'}, use_global_device_ids=true, to_apply=%add | all-reduce | flops 2048 | bytes 8192
  98.5 81.0 %all-gather.3.cloned.1.call-done = bf16[2048,2048]{1,0:T(8,128)(2,1)} async-done(((bf16[256,2048]{1,0:T(8,128)(2,1)}), bf16[2048,2048]{1,0:T(8,128)(2,1)}) %all-gather.3.cloned.1.call-update) | async-done | bytes 8388624 | tf_op jit(solution)/shard_map/all_gather | solution.py:18
  179.5 125.4 %all-gather.5.cloned.1.call-done = bf16[2048,2048]{1,0:T(8,128)(2,1)} async-done(((bf16[256,2048]{1,0:T(8,128)(2,1)}), bf16[2048,2048]{1,0:T(8,128)(2,1)}) %all-gather.5.cloned.1.call-update) | async-done | bytes 8388624 | tf_op jit(solution)/shard_map/all_gather | solution.py:19
  304.9 8.4 %copy.15 = bf16[2048,2048]{1,0:T(8,128)(2,1)} copy(bf16[2048,2048]{1,0:T(8,128)(2,1)} %all-gather.3.cloned.1.call-done) | data formatting | bytes 16777216
  313.3 8.4 %copy.16 = bf16[2048,2048]{1,0:T(8,128)(2,1)} copy(bf16[2048,2048]{1,0:T(8,128)(2,1)} %all-gather.5.cloned.1.call-done) | data formatting | bytes 16777216
  (2 shorter events, 0.0 us)
Async XLA Ops:
  7.2 172.3 %all-gather.3.cloned.1.call-start = ((), (), s32[]{:S(2)}) async-start(), calls=%async_computation | async-start | bytes 9437184 | tf_op jit(solution)/shard_map/all_gather | solution.py:18
  7.9 43.3 %copy-start = (f32[256,2048]{1,0:T(8,128)S(1)}, f32[256,2048]{1,0:T(8,128)}, u32[]{:S(2)}) copy-start(f32[256,2048]{1,0:T(8,128)} %param.10) | copy-start | bytes 6291460
  7.9 43.3 %copy-start.1 = (f32[256]{0:T(256)S(1)}, f32[256]{0:T(256)}, u32[]{:S(2)}) copy-start(f32[256]{0:T(256)} %param.11) | copy-start | bytes 3076
  51.1 5.4 %copy-start.2 = (f32[2048]{0:T(1024)}, f32[2048]{0:T(1024)S(1)}, u32[]{:S(2)}) copy-start(f32[2048]{0:T(1024)S(1)} %get-tuple-element.18) | copy-start | bytes 24580
  51.1 5.4 %copy-start.3 = (f32[2048]{0:T(1024)}, f32[2048]{0:T(1024)S(1)}, u32[]{:S(2)}) copy-start(f32[2048]{0:T(1024)S(1)} %get-tuple-element.19) | copy-start | bytes 24580
  56.5 0.8 copy-start.4
  56.5 0.8 copy-start.5
  56.6 248.3 %all-gather.5.cloned.1.call-start = ((), (), s32[]{:S(2)}) async-start(), calls=%async_computation.1 | async-start | bytes 9437184 | tf_op jit(solution)/shard_map/all_gather | solution.py:19
Sparse Core Ops, SparseCore 0:
  56.7 122.7 all-gather.2
  182.2 122.6 all-gather.4
where the time goes:
time: 329 us
  waiting for transfers between devices  207 us (63%)
  blocking collectives  79.8 us (24%)
  local copies, waits for them, and re-layouts  17.2 us (5%)
  between operations  14.1 us (4%)
  other arithmetic  10.4 us (3%)
    all_gather x1, waiting for transfers between devices, local(): lax.all_gather(narrow_up, 'shard', axis=0, tiled=True)  125 us
    all_gather x1, waiting for transfers between devices, local(): lax.all_gather(narrow_gate, 'shard', axis=0, tiled=True)  81 us
    unnamed x1, blocking collectives  40.9 us
    pmax x1, blocking collectives, local(): lax.pmax((jnp.max(jnp.abs(result_gate), axis=0), jnp.max(jnp.abs(result_u...  38.9 us
    unnamed x16, local copies, waits for them, and re-layouts  17.2 us
  transfers between devices with their start and end apart: 2, of which 2 were waited for; matrix products, arithmetic and copies ran while one was open for 0% of the time, Pallas kernels for 0%

commit v1 on v0

v1 whole, which is shorter than its diff:
```python
import functools

import jax
import jax.numpy as jnp
from jax import lax
from jax.experimental import pallas as pl
from jax.experimental.pallas import tpu as pltpu
from jax.sharding import PartitionSpec as P

MESH = pl.DeviceIdType.MESH
LANES = 128


def position_of(index, n):
    return jnp.where(index % 2 == 0, index // 2, n - 1 - index // 2)


def index_at(position, n):
    return jnp.where(position < n // 2, 2 * position, 2 * (n - 1 - position) + 1)


def kernel(
    n, k, parts,
    one_gate, other_gate, one_up, other_up, mix, norm_train, norm_step,
    final_gate, final_up, column_gate, column_up, serve_norm,
    held_one, held_other, share, maxima_gate, maxima_up, gains,
    load_sem, max_send, max_recv, norm_send, norm_recv, ring_send, ring_recv,
):
    rows, cols = one_gate.shape
    piece = norm_train.shape[1]
    part = rows // parts
    me, col = lax.axis_index("shard"), lax.axis_index("model")
    at = position_of(me, n)

    ones, others = (one_gate, one_up), (other_gate, other_up)
    finals, columns, maxima = (final_gate, final_up), (column_gate, column_up), (maxima_gate, maxima_up)

    loads = {}
    for w in range(2):
        for c in range(parts):
            span = pl.ds(c * part, part)
            pair = (
                pltpu.make_async_copy(ones[w].at[span], held_one.at[w, span], load_sem.at[w, c, 0]),
                pltpu.make_async_copy(others[w].at[span], held_other.at[w, span], load_sem.at[w, c, 1]),
            )
            for copy in pair:
                copy.start()
            loads[w, c] = pair

    barrier = pltpu.get_barrier_semaphore()
    for d in range(1, n):
        pl.semaphore_signal(barrier, inc=1, device_id=((me + d) % n, col), device_id_type=MESH)
    for d in range(1, k):
        pl.semaphore_signal(barrier, inc=1, device_id=(me, (col + d) % k), device_id_type=MESH)

    share[...] = jnp.broadcast_to(mix[...], (LANES, rows)).T

    maxima_up[0, :, cols:cols + piece] = norm_train[...] + norm_step[...]

    def mixed(w):
        top = jnp.zeros((8, cols), jnp.float32)
        for c in range(parts):
            for copy in loads[w, c]:
                copy.wait()

            def step(g, top):
                span = pl.ds(pl.multiple_of(c * part + g * 8, 8), 8)
                m = share[span, 0:1]
                result = m * held_one[w, span, :] + (1.0 - m) * held_other[w, span, :]
                held_one[w, span, :] = result
                return jnp.maximum(top, jnp.abs(result))

            top = lax.fori_loop(0, part // 8, step, top, unroll=2)
        maxima[w][0, :, 0:cols] = jnp.max(top, axis=0, keepdims=True)

    def tell(w):
        copies = []
        for d in range(1, n):
            copy = pltpu.make_async_remote_copy(
                src_ref=maxima[w].at[0], dst_ref=maxima[w].at[d],
                send_sem=max_send.at[w, d], recv_sem=max_recv.at[w, d],
                device_id=((me + d) % n, col), device_id_type=MESH,
            )
            copy.start()
            copies.append(copy)
        return copies

    def ring(way, hop, w, c):
        origin = index_at((at + (n - hop if way == 0 else hop)) % n, n)
        span = pl.ds(pl.multiple_of(origin * rows + c * part, part), part)
        to = index_at((at + (1 if way == 0 else n - 1)) % n, n)
        return pltpu.make_async_remote_copy(
            src_ref=finals[w].at[span], dst_ref=finals[w].at[span],
            send_sem=ring_send.at[way, hop, w, c], recv_sem=ring_recv.at[way, hop, w, c],
            device_id=(to, col), device_id_type=MESH,
        )

    def scaled(w, c, inverse):
        def step(g, _):
            start = pl.multiple_of(c * part + g * 16, 16)
            to = pl.multiple_of(me * rows + c * part + g * 16, 16)
            finals[w][pl.ds(to, 16), :] = (held_one[w, pl.ds(start, 16), :] * inverse).astype(jnp.bfloat16)
            return 0

        lax.fori_loop(0, part // 16, step, 0)

    mixed(0)
    pl.semaphore_wait(barrier, n - 1 + k - 1)
    told = [tell(0)]
    mixed(1)
    told.append(tell(1))

    sent, norms = {}, []
    for w in range(2):
        for copy in told[w]:
            copy.wait_recv()
        column = jnp.max(maxima[w][:, :, 0:cols], axis=0)
        columns[w][...] = column
        inverse = 1.0 / column
        for c in range(parts):
            scaled(w, c, inverse)
            for way in range(2):
                sent[way, 0, w, c] = ring(way, 0, w, c)
                sent[way, 0, w, c].start()

    for d in range(n):
        gains[0, pl.ds((me + (n - d)) % n, 1), :] = maxima_up[d, :, cols:cols + LANES]
    for d in range(1, k):
        copy = pltpu.make_async_remote_copy(
            src_ref=gains.at[0], dst_ref=gains.at[d],
            send_sem=norm_send.at[d], recv_sem=norm_recv.at[d],
            device_id=(me, (col + d) % k), device_id_type=MESH,
        )
        copy.start()
        norms.append(copy)
    for copy in norms:
        copy.wait_recv()
    serve_norm[...] = jnp.concatenate(
        [gains[(col + (k - j)) % k][:, 0:piece] for j in range(k)], axis=1
    ).astype(jnp.bfloat16)

    for hop in range(1, n // 2 + 1):
        for w in range(2):
            for c in range(parts):
                for way in range(2):
                    if (way, hop - 1, w, c) not in sent:
                        continue
                    sent[way, hop - 1, w, c].wait_recv()
                    if hop < n // 2 - 1 or (hop == n // 2 - 1 and way == w):
                        sent[way, hop, w, c] = ring(way, hop, w, c)
                        sent[way, hop, w, c].start()

    for copy in sent.values():
        copy.wait_send()
    for copy in told[0] + told[1] + norms:
        copy.wait_send()


def solution(mesh):
    n, k = mesh.shape["shard"], mesh.shape["model"]

    def local(one_gate, other_gate, one_up, other_up, mix_share, norm_train, norm_step):
        rows, cols = one_gate.shape
        piece = norm_train.shape[0]
        parts = 4 if n <= 8 else 1
        whole = jax.ShapeDtypeStruct if n > 8 else pltpu.VMEM
        hbm, vmem = pl.BlockSpec(memory_space=pltpu.HBM), pl.BlockSpec(memory_space=pltpu.VMEM)
        final_gate, final_up, column_gate, column_up, serve_norm = pl.pallas_call(
            functools.partial(kernel, n, k, parts),
            out_shape=[
                whole((n * rows, cols), jnp.bfloat16),
                whole((n * rows, cols), jnp.bfloat16),
                jax.ShapeDtypeStruct((1, cols), jnp.float32),
                jax.ShapeDtypeStruct((1, cols), jnp.float32),
                jax.ShapeDtypeStruct((n, k * piece), jnp.bfloat16),
            ],
            in_specs=[hbm] * 4 + [vmem] * 3,
            out_specs=[vmem] * 5,
            scratch_shapes=[
                pltpu.VMEM((2, rows, cols), jnp.float32),
                pltpu.VMEM((2, rows, cols), jnp.float32),
                pltpu.VMEM((rows, LANES), jnp.float32),
                pltpu.VMEM((n, 1, cols), jnp.float32),
                pltpu.VMEM((n, 1, cols + LANES), jnp.float32),
                pltpu.VMEM((k, n, LANES), jnp.float32),
                pltpu.SemaphoreType.DMA((2, parts, 2)),
                pltpu.SemaphoreType.DMA((2, n)),
                pltpu.SemaphoreType.DMA((2, n)),
                pltpu.SemaphoreType.DMA((k,)),
                pltpu.SemaphoreType.DMA((k,)),
                pltpu.SemaphoreType.DMA((2, n // 2, 2, parts)),
                pltpu.SemaphoreType.DMA((2, n // 2, 2, parts)),
            ],
            compiler_params=pltpu.CompilerParams(
                collective_id=0, has_side_effects=True, vmem_limit_bytes=46 * 2**20
            ),
        )(
            one_gate, other_gate, one_up, other_up,
            mix_share.reshape(1, rows), norm_train.reshape(1, piece), norm_step.reshape(1, piece),
        )
        return (
            final_gate, final_up, column_gate.reshape(cols), column_up.reshape(cols),
            serve_norm.reshape(n * k * piece),
        )

    return jax.shard_map(
        local,
        mesh=mesh,
        in_specs=(
            P("shard", "model"), P("shard", "model"), P("shard", "model"), P("shard", "model"),
            P("shard"), P(("shard", "model")), P(("shard", "model")),
        ),
        out_specs=(P(None, "model"), P(None, "model"), P("model"), P("model"), P()),
        check_vma=False,
    )
```

time: 329 us -> 181 us (0.55)
  waiting for transfers between devices: 207 us -> 0 us
  Pallas kernels: 0 us -> 172 us
  blocking collectives: 79.8 us -> 0 us
  between operations: 14.1 us -> 0.65 us
  other arithmetic: 10.4 us -> 0 us
  local copies, waits for them, and re-layouts: 17.2 us -> 8.6 us
    all_gather x2 -> x0, waiting for transfers between devices: 206 us -> none  [the longest x1 125 us: local(): lax.all_gather(narrow_up, 'shard', axis=0, tiled=True)]
    pallas_call x0 -> x1, Pallas kernels: none -> 172 us  [local(): pl.pallas_call(functools.partial(kernel, n, k, parts), out_shape=[whole((...]
    unnamed x1 -> x0, blocking collectives: 40.9 us -> none
    pmax x1 -> x0, blocking collectives: 38.9 us -> none  [local(): lax.pmax((jnp.max(jnp.abs(result_gate), axis=0), jnp.max(jnp.abs(result_u...]
    unnamed x16 -> x11, local copies, waits for them, and re-layouts: 17.2 us -> 8.6 us
    convert_element_type x2 -> x0, other arithmetic: 5.36 us -> none  [the longest x1 5.36 us: local(): (result_up / column_up).astype(jnp.bfloat16)]
    reduce_max x1 -> x0, other arithmetic: 4.36 us -> none  [local(): jnp.max(jnp.abs(result_up), axis=0)]
  transfers between devices with their start and end apart: 2 -> 0, of which waited for: 2 -> 0; matrix products, arithmetic and copies ran while one was open for 0% -> 0% of each run, Pallas kernels for 0% -> 0%
where the time goes in v1:
time: 181 us
  Pallas kernels  172 us (95%)
  local copies, waits for them, and re-layouts  8.6 us (5%)
    pallas_call x1, Pallas kernels, local(): pl.pallas_call(functools.partial(kernel, n, k, parts), out_shape=[whole((...  172 us
    unnamed x11, local copies, waits for them, and re-layouts  8.6 us

profile of v1, /device:TPU:0, one launch (start us, length us, event | category | flops | bytes accessed | tf_op | source)
XLA Modules:
  0.0 180.8 jit_solution(5460961339282765732)
XLA Ops:
  0.6 171.6 %shard_map.110 = (bf16[2048,2048]{1,0:T(8,128)(2,1)S(1)}, bf16[2048,2048]{1,0:T(8,128)(2,1)S(1)}, f32[1,2048]{1,0:T(1,128)}, f32[1,2048]{1,0:T(1,128)}, bf16[8,256]{1,0:T(8,128)(2,1)}) custom-call(f32[256,2048]{1,0:T(8,128)} %one_gate.1, f32[256,2048]{1,0:T(8,128)} %other_gate.1, f32[256,2048]{1,0:T(8,128)} %one_up.1, f32[256,2048]{1,0:T(8,128)} %other_up.1, ...), custom_call_target="tpu_custom_call" | custom-call | tf_op jit(solution)/shard_map/pallas_call | solution.py:168
  172.2 0.0 copy-start.2
  172.2 3.4 %copy.17 = bf16[2048,2048]{1,0:T(8,128)(2,1)} copy(bf16[2048,2048]{1,0:T(8,128)(2,1)S(1)} %get-tuple-element.15) | data formatting | bytes 16777216
  175.6 0.0 copy-done.2
  175.6 0.6 copy.12
  176.2 0.0 copy-start.1
  176.2 0.0 copy-start
  176.2 3.4 %copy.18 = bf16[2048,2048]{1,0:T(8,128)(2,1)} copy(bf16[2048,2048]{1,0:T(8,128)(2,1)S(1)} %get-tuple-element.16) | data formatting | bytes 16777216
  179.6 0.0 copy-done.1
  179.6 0.6 copy.19
  180.2 0.0 copy-done
  180.2 0.6 copy.20
Async XLA Ops:
  172.2 3.4 %copy-start.2 = (bf16[8,256]{1,0:T(8,128)(2,1)S(1)}, bf16[8,256]{1,0:T(8,128)(2,1)}, u32[]{:S(2)}) copy-start(bf16[8,256]{1,0:T(8,128)(2,1)} %get-tuple-element.14) | copy-start | bytes 12292
  176.2 3.4 %copy-start.1 = (f32[1,2048]{1,0:T(1,128)S(1)}, f32[1,2048]{1,0:T(1,128)}, u32[]{:S(2)}) copy-start(f32[1,2048]{1,0:T(1,128)} %get-tuple-element.12) | copy-start | bytes 24580
  176.2 4.0 %copy-start = (f32[1,2048]{1,0:T(1,128)S(1)}, f32[1,2048]{1,0:T(1,128)}, u32[]{:S(2)}) copy-start(f32[1,2048]{1,0:T(1,128)} %get-tuple-element.13) | copy-start | bytes 24580

commit v2 on v1

v2 whole, which is shorter than its diff:
```python
import functools

import jax
import jax.numpy as jnp
from jax import lax
from jax.experimental import pallas as pl
from jax.experimental.pallas import tpu as pltpu
from jax.sharding import PartitionSpec as P

MESH = pl.DeviceIdType.MESH
LANES = 128


def position_of(index, n):
    return jnp.where(index % 2 == 0, index // 2, n - 1 - index // 2)


def index_at(position, n):
    return jnp.where(position < n // 2, 2 * position, 2 * (n - 1 - position) + 1)


def kernel(
    n, k, parts,
    one_gate, other_gate, one_up, other_up, mix, norm_train, norm_step,
    final_gate, final_up, column_gate, column_up, serve_norm,
    held_one, held_other, share, maxima, gains, gain_rows,
    load_sem, max_send, max_recv, norm_send, norm_recv, ring_send, ring_recv,
):
    rows, cols = one_gate.shape
    piece = norm_train.shape[1]
    part = cols // parts
    me, col = lax.axis_index("shard"), lax.axis_index("model")
    at = position_of(me, n)

    ones, others = (one_gate, one_up), (other_gate, other_up)
    finals, columns = (final_gate, final_up), (column_gate, column_up)

    loads = {}
    for w in range(2):
        for c in range(parts):
            span = pl.ds(c * part, part)
            pair = (
                pltpu.make_async_copy(ones[w].at[:, span], held_one.at[w, :, span], load_sem.at[w, c, 0]),
                pltpu.make_async_copy(others[w].at[:, span], held_other.at[w, :, span], load_sem.at[w, c, 1]),
            )
            for copy in pair:
                copy.start()
            loads[w, c] = pair

    barrier = pltpu.get_barrier_semaphore()
    for d in range(1, n):
        pl.semaphore_signal(barrier, inc=1, device_id=((me + d) % n, col), device_id_type=MESH)
    for d in range(1, k):
        pl.semaphore_signal(barrier, inc=1, device_id=(me, (col + d) % k), device_id_type=MESH)

    share[...] = jnp.broadcast_to(mix[...], (LANES, rows)).T

    maxima[1, parts - 1, 0, :, part:part + piece] = norm_train[...] + norm_step[...]

    def mixed(w, c):
        for copy in loads[w, c]:
            copy.wait()
        span = pl.ds(c * part, part)

        def step(g, top):
            lines = pl.ds(pl.multiple_of(g * 8, 8), 8)
            m = share[lines, 0:1]
            result = m * held_one[w, lines, span] + (1.0 - m) * held_other[w, lines, span]
            held_one[w, lines, span] = result
            return jnp.maximum(top, jnp.abs(result))

        top = lax.fori_loop(0, rows // 8, step, jnp.zeros((8, part), jnp.float32), unroll=4)
        maxima[w, c, 0, :, 0:part] = jnp.max(top, axis=0, keepdims=True)

    def tell(w, c):
        width = part + LANES if (w, c) == (1, parts - 1) else part
        copies = []
        for d in range(1, n):
            copy = pltpu.make_async_remote_copy(
                src_ref=maxima.at[w, c, 0, :, pl.ds(0, width)], dst_ref=maxima.at[w, c, d, :, pl.ds(0, width)],
                send_sem=max_send.at[w, c, d], recv_sem=max_recv.at[w, c, d],
                device_id=((me + d) % n, col), device_id_type=MESH,
            )
            copy.start()
            copies.append(copy)
        return copies

    def ring(way, hop, w, c):
        origin = index_at((at + (n - hop if way == 0 else hop)) % n, n)
        lines, span = pl.ds(pl.multiple_of(origin * rows, rows), rows), pl.ds(c * part, part)
        to = index_at((at + (1 if way == 0 else n - 1)) % n, n)
        return pltpu.make_async_remote_copy(
            src_ref=finals[w].at[lines, span], dst_ref=finals[w].at[lines, span],
            send_sem=ring_send.at[way, hop, w, c], recv_sem=ring_recv.at[way, hop, w, c],
            device_id=(to, col), device_id_type=MESH,
        )

    def scaled(w, c, inverse):
        span = pl.ds(c * part, part)

        def step(g, _):
            start = pl.multiple_of(g * 16, 16)
            to = pl.multiple_of(me * rows + g * 16, 16)
            finals[w][pl.ds(to, 16), span] = (held_one[w, pl.ds(start, 16), span] * inverse).astype(jnp.bfloat16)
            return 0

        lax.fori_loop(0, rows // 16, step, 0, unroll=2)

    units = [(w, c) for w in range(2) for c in range(parts)]
    told = {}
    for w, c in units:
        mixed(w, c)
        if (w, c) == units[0]:
            pl.semaphore_wait(barrier, n - 1 + k - 1)
        told[w, c] = tell(w, c)

    sent, norms = {}, []
    for w, c in units:
        for copy in told[w, c]:
            copy.wait_recv()
        column = jnp.max(maxima[w, c, :, :, 0:part], axis=0)
        columns[w][:, pl.ds(c * part, part)] = column
        scaled(w, c, 1.0 / column)
        for way in range(2):
            sent[way, 0, w, c] = ring(way, 0, w, c)
            sent[way, 0, w, c].start()

    for d in range(n):
        gains[0, pl.ds((me + (n - d)) % n, 1), :] = maxima[1, parts - 1, d, :, part:part + LANES]
    for d in range(1, k):
        copy = pltpu.make_async_remote_copy(
            src_ref=gains.at[0], dst_ref=gains.at[d],
            send_sem=norm_send.at[d], recv_sem=norm_recv.at[d],
            device_id=(me, (col + d) % k), device_id_type=MESH,
        )
        copy.start()
        norms.append(copy)
    for copy in norms:
        copy.wait_recv()
    gain = jnp.concatenate([gains[(col + (k - j)) % k][:, 0:piece] for j in range(k)], axis=1)
    if serve_norm.shape[1] == gain.shape[1]:
        serve_norm[...] = gain.astype(jnp.bfloat16)
    else:
        each = k * piece // LANES
        for i in range(n * each):
            at_lane = i % each * LANES
            gain_rows[i:i + 1, :] = gain[i // each:i // each + 1, at_lane:at_lane + LANES]
        serve_norm[...] = gain_rows[...].astype(jnp.bfloat16)

    for hop in range(1, n // 2 + 1):
        for w in range(2):
            for c in range(parts):
                for way in range(2):
                    if (way, hop - 1, w, c) not in sent:
                        continue
                    sent[way, hop - 1, w, c].wait_recv()
                    if hop < n // 2 - 1 or (hop == n // 2 - 1 and way == w):
                        sent[way, hop, w, c] = ring(way, hop, w, c)
                        sent[way, hop, w, c].start()

    for copy in sent.values():
        copy.wait_send()
    for copy in sum(told.values(), norms):
        copy.wait_send()


def writer(*refs):
    (sem,), count = refs[-1:], (len(refs) - 1) // 2
    copies = []
    for source, target in zip(refs[:count], refs[count:-1]):
        pieces = 4 if source.shape[0] > LANES else 1
        lines = source.shape[0] // pieces
        for p in range(pieces):
            span = pl.ds(p * lines, lines)
            copies.append(pltpu.make_async_copy(source.at[span], target.at[span], sem.at[len(copies)]))
    for copy in copies:
        copy.start()
    for copy in copies:
        copy.wait()


def solution(mesh):
    n, k = mesh.shape["shard"], mesh.shape["model"]

    def local(one_gate, other_gate, one_up, other_up, mix_share, norm_train, norm_step):
        rows, cols = one_gate.shape
        piece = norm_train.shape[0]
        parts = 2 if n <= 8 else 1
        near = n <= 8
        shaped = pltpu.VMEM if near else jax.ShapeDtypeStruct
        norm_shape = (n * k * piece // LANES, LANES) if k * piece % LANES == 0 else (n, k * piece)
        shapes = [
            ((n * rows, cols), jnp.bfloat16), ((n * rows, cols), jnp.bfloat16),
            ((1, cols), jnp.float32), ((1, cols), jnp.float32), (norm_shape, jnp.bfloat16),
        ]
        hbm, vmem = pl.BlockSpec(memory_space=pltpu.HBM), pl.BlockSpec(memory_space=pltpu.VMEM)
        results = pl.pallas_call(
            functools.partial(kernel, n, k, parts),
            out_shape=[shaped(*shape) for shape in shapes],
            in_specs=[hbm] * 4 + [vmem] * 3,
            out_specs=[vmem] * 5,
            scratch_shapes=[
                pltpu.VMEM((2, rows, cols), jnp.float32),
                pltpu.VMEM((2, rows, cols), jnp.float32),
                pltpu.VMEM((rows, LANES), jnp.float32),
                pltpu.VMEM((2, parts, n, 1, cols // parts + LANES), jnp.float32),
                pltpu.VMEM((k, n, LANES), jnp.float32),
                pltpu.VMEM((max(n * k * piece // LANES, 8), LANES), jnp.float32),
                pltpu.SemaphoreType.DMA((2, parts, 2)),
                pltpu.SemaphoreType.DMA((2, parts, n)),
                pltpu.SemaphoreType.DMA((2, parts, n)),
                pltpu.SemaphoreType.DMA((k,)),
                pltpu.SemaphoreType.DMA((k,)),
                pltpu.SemaphoreType.DMA((2, n // 2, 2, parts)),
                pltpu.SemaphoreType.DMA((2, n // 2, 2, parts)),
            ],
            compiler_params=pltpu.CompilerParams(
                collective_id=0, has_side_effects=True, vmem_limit_bytes=46 * 2**20
            ),
        )(
            one_gate, other_gate, one_up, other_up,
            mix_share.reshape(1, rows), norm_train.reshape(1, piece), norm_step.reshape(1, piece),
        )
        if near:
            results = pl.pallas_call(
                writer,
                out_shape=[jax.ShapeDtypeStruct(*shape) for shape in shapes],
                in_specs=[vmem] * 5,
                out_specs=[hbm] * 5,
                scratch_shapes=[pltpu.SemaphoreType.DMA((11,))],
                compiler_params=pltpu.CompilerParams(vmem_limit_bytes=2**20),
            )(*results)
        final_gate, final_up, column_gate, column_up, serve_norm = results
        return (
            final_gate, final_up, column_gate.reshape(cols), column_up.reshape(cols),
            serve_norm.reshape(n * k * piece),
        )

    return jax.shard_map(
        local,
        mesh=mesh,
        in_specs=(
            P("shard", "model"), P("shard", "model"), P("shard", "model"), P("shard", "model"),
            P("shard"), P(("shard", "model")), P(("shard", "model")),
        ),
        out_specs=(P(None, "model"), P(None, "model"), P("model"), P("model"), P()),
        check_vma=False,
    )
```

time: 181 us -> 177 us (0.978)
  local copies, waits for them, and re-layouts: 8.6 us -> 0 us
  Pallas kernels: 172 us -> 176 us
    unnamed x11 -> x0, local copies, waits for them, and re-layouts: 8.6 us -> none
    pallas_call x1 -> x2, Pallas kernels: 172 us -> 176 us  [the longest x1 170 us: local(): pl.pallas_call(functools.partial(kernel, n, k, parts), out_shape=[shaped(...]
where the time goes in v2:
time: 177 us
  Pallas kernels  176 us (99%)
    pallas_call x1, Pallas kernels, local(): pl.pallas_call(functools.partial(kernel, n, k, parts), out_shape=[shaped(...  170 us
    pallas_call x1, Pallas kernels, local(): pl.pallas_call(writer, out_shape=[jax.ShapeDtypeStruct(*shape) for shape...  5.96 us

profile of v2, /device:TPU:0, one launch (start us, length us, event | category | flops | bytes accessed | tf_op | source)
XLA Modules:
  0.0 176.9 jit_solution(10208702115904466838)
XLA Ops:
  0.6 170.3 %shard_map.110 = (bf16[2048,2048]{1,0:T(8,128)(2,1)S(1)}, bf16[2048,2048]{1,0:T(8,128)(2,1)S(1)}, f32[1,2048]{1,0:T(1,128)S(1)}, f32[1,2048]{1,0:T(1,128)S(1)}, bf16[16,128]{1,0:T(8,128)(2,1)S(1)}) custom-call(f32[256,2048]{1,0:T(8,128)} %one_gate.1, f32[256,2048]{1,0:T(8,128)} %other_gate.1, f32[256,2048]{1,0:T(8,128)} %one_up.1, f32[256,2048]{1,0:T(8,128)} %other_up.1, ...), custom_call_target="tpu_custom_call" | custom-call | tf_op jit(solution)/shard_map/pallas_call | solution.py:197
  171.0 6.0 %shard_map.111 = (bf16[2048,2048]{1,0:T(8,128)(2,1)}, bf16[2048,2048]{1,0:T(8,128)(2,1)}, f32[1,2048]{1,0:T(1,128)}, f32[1,2048]{1,0:T(1,128)}, bf16[16,128]{1,0:T(8,128)(2,1)}) custom-call(bf16[2048,2048]{1,0:T(8,128)(2,1)S(1)} %get-tuple-element.15.refs_0_, bf16[2048,2048]{1,0:T(8,128)(2,1)S(1)} %get-tuple-element.16.refs_1_, ...), custom_call_target="tpu_custom_call" | custom-call | tf_op jit(solution)/shard_map/pallas_call | solution.py:225
